TPU v7x, 32 devices: a whole 2x2x4 slice. The times are simulated.
32 devices in a mesh: gx: 4 (over x, core), gy: 8 (over z, y).
Axes of the slice: x: 2, y: 2, z: 4, core: 2. Of those that a mesh axis runs over, the one named last changes fastest.
Arguments:
- midpoints: float32 [4, 8, 64, 3, 256], P('gx', 'gy'), may hold values from 0 to 1
- halves: float32 [4, 8, 64, 3, 256], P('gx', 'gy'), may hold values from -0.3 to 0.3
- burgers: float32 [4, 8, 64, 3, 256], P('gx', 'gy'), may hold values from -6 to 6
- mobility: float32 [4, 8, 64, 256], P('gx', 'gy'), may hold values from 0.5 to 2
- pair_left: int32 [4, 8, 128], P('gx', 'gy'), may hold values from 0 to 63
- pair_right: int32 [4, 8, 128], P('gx', 'gy'), may hold values from 0 to 63
- pair_slot: int32 [4, 8, 128], P('gx', 'gy'), may hold values from 0 to 4
- pair_count: int32 [4, 8], P('gx', 'gy'), may hold values from 1 to 128, as said below
Outputs:
- final_midpoints: float32 [4, 8, 64, 3, 256], P('gx', 'gy')
- corrector_force: float32 [4, 8, 64, 3, 256], P('gx', 'gy')
Inputs may be any that keep to these rules, and one draw needn't show every extreme that they name: `pair_count`: slots at or beyond a device's count hold valid indices that are no pairs. In every draw some device has exactly 128 pairs.
All inputs are finite; a program needn't handle non-finite values.
Results may differ from a plain program's by a relative error of at most 0.0003.
Values sent between devices are 32-bit elements; how exact they have to be, the bound alone decides.
A program may use at most 128 MiB of HBM per device.

v0:
```python
import jax
import jax.numpy as jnp
from jax import lax
from jax.sharding import PartitionSpec as P

core_square = 0.04
poisson_part = 0.6
time_step = 0.1
gauss_offset = 0.5773502691896258
east_steps = (0, 1, 0, 1, 1)
north_steps = (0, 0, 1, 1, -1)


def from_behind(x, axis, by):
    devices = lax.axis_size(axis)
    return lax.ppermute(x, axis, [(i, (i + by) % devices) for i in range(devices)])


def pair_forces(mid_a, half_a, burg_a, mid_b, half_b, burg_b, offset):
    burg_dot = jnp.einsum("...ci,...cj->...ij", burg_a, burg_b, precision=lax.Precision.HIGHEST)
    half_dot = jnp.einsum("...ci,...cj->...ij", half_a, half_b, precision=lax.Precision.HIGHEST)
    screw_a = jnp.sum(burg_a * half_a, axis=-2)
    screw_b = jnp.sum(burg_b * half_b, axis=-2)
    coupling = 4.0 * (
        burg_dot * half_dot + poisson_part * screw_a[..., :, None] * screw_b[..., None, :]
    )
    force_a = jnp.zeros_like(mid_a)
    force_b = jnp.zeros_like(mid_b)
    for sign_a in (1.0, -1.0):
        for sign_b in (1.0, -1.0):
            point_a = mid_a + sign_a * gauss_offset * half_a
            point_b = mid_b + offset + sign_b * gauss_offset * half_b
            pieces = [
                point_a[..., component, :, None] - point_b[..., component, None, :]
                for component in range(3)
            ]
            distance = (
                core_square + pieces[0] * pieces[0] + pieces[1] * pieces[1] + pieces[2] * pieces[2]
            )
            inverse = 1.0 / jnp.sqrt(distance)
            kernel = (
                0.25
                * coupling
                * inverse
                * inverse
                * inverse
                * (1.0 + 1.5 * core_square * inverse * inverse)
            )
            force_a = force_a + jnp.stack(
                [jnp.sum(kernel * piece, axis=-1) for piece in pieces], axis=-2
            )
            force_b = force_b - jnp.stack(
                [jnp.sum(kernel * piece, axis=-2) for piece in pieces], axis=-2
            )
    return (force_a, force_b)


def slot_offsets(slot_rows):
    shift_x = jnp.zeros(slot_rows.shape, jnp.float32)
    shift_y = jnp.zeros(slot_rows.shape, jnp.float32)
    for number in range(5):
        shift_x = shift_x + jnp.where(slot_rows == number, float(east_steps[number]), 0.0)
        shift_y = shift_y + jnp.where(slot_rows == number, float(north_steps[number]), 0.0)
    return jnp.stack([shift_x, shift_y, jnp.zeros_like(shift_x)], axis=-1)[..., None]


def table_place(slot_rows, layout):
    placed = jnp.zeros_like(slot_rows)
    for number in range(5):
        placed = placed + jnp.where(slot_rows == number, layout[number], 0)
    return placed


def split_rows(rows):
    return (rows[:, :3], rows[:, 3:6], rows[:, 6:])


def gather_near(blocks):
    eastern = from_behind(blocks, "gx", -1)
    northern = from_behind(jnp.stack([blocks, eastern]), "gy", -1)
    southern = from_behind(eastern, "gy", 1)
    return jnp.stack([blocks, eastern, northern[0], northern[1], southern])


def own_sweep(own_blocks, near_table, left_rows, right_rows, slot_rows, live_count):
    block_count = own_blocks.shape[0]
    segments = own_blocks.shape[2]
    group_size = min(8, left_rows.shape[0])
    layout = (0, 1, 2, 3, 4)
    flat_table = near_table.reshape((-1,) + near_table.shape[2:])
    columns = jnp.arange(block_count, dtype=jnp.int32)
    back_columns = jnp.arange(4 * block_count, dtype=jnp.int32)

    def advance(number, running):
        begin_at = number * group_size
        first_ids = lax.dynamic_slice_in_dim(left_rows, begin_at, group_size)
        second_ids = lax.dynamic_slice_in_dim(right_rows, begin_at, group_size)
        kinds = lax.dynamic_slice_in_dim(slot_rows, begin_at, group_size)
        first_rows = jnp.take(own_blocks, first_ids, axis=0)
        second_rows = jnp.take(
            flat_table, table_place(kinds, layout) * block_count + second_ids, axis=0
        )
        mid_a, half_a, burg_a = split_rows(first_rows)
        mid_b, half_b, burg_b = split_rows(second_rows)
        force_a, force_b = pair_forces(
            mid_a, half_a, burg_a, mid_b, half_b, burg_b, slot_offsets(kinds)
        )
        active = (begin_at + jnp.arange(group_size, dtype=jnp.int32) < live_count).astype(
            jnp.float32
        )
        inside = jnp.where((kinds == 0) & (first_ids != second_ids), active, 0.0)
        hot_a = jnp.where(first_ids[:, None] == columns[None, :], active[:, None], 0.0)
        hot_b = jnp.where(second_ids[:, None] == columns[None, :], inside[:, None], 0.0)
        own_sum = running[0] + jnp.einsum(
            "gb,gcs->bcs", hot_a, force_a, precision=lax.Precision.HIGHEST
        )
        own_sum = own_sum + jnp.einsum(
            "gb,gcs->bcs", hot_b, force_b, precision=lax.Precision.HIGHEST
        )
        outward = jnp.where(kinds > 0, active, 0.0)
        hot_back = jnp.where(
            ((kinds - 1) * block_count + second_ids)[:, None] == back_columns[None, :],
            outward[:, None],
            0.0,
        )
        return (
            own_sum,
            running[1]
            + jnp.einsum("gb,gcs->bcs", hot_back, force_b, precision=lax.Precision.HIGHEST),
        )

    starting = (
        jnp.zeros((block_count, 3, segments), jnp.float32),
        jnp.zeros((4 * block_count, 3, segments), jnp.float32),
    )
    rounds = (live_count + group_size - 1) // group_size
    return lax.fori_loop(0, rounds, advance, starting)


def give_back(back_forces, block_count):
    pieces = back_forces.reshape((4, block_count) + back_forces.shape[1:])
    northern = from_behind(jnp.stack([pieces[1], pieces[2]]), "gy", 1)
    southern = from_behind(pieces[3], "gy", -1)
    eastern = from_behind(pieces[0] + northern[1] + southern, "gx", 1)
    return northern[0] + eastern


def evaluate(own_blocks, near_table, left_rows, right_rows, slot_rows, live_count):
    own_sum, back_forces = own_sweep(
        own_blocks, near_table, left_rows, right_rows, slot_rows, live_count
    )
    return own_sum + give_back(back_forces, own_blocks.shape[0])


def on_device(midpoints, halves, burgers, mobility, pair_left, pair_right, pair_slot, pair_count):
    middles = midpoints[0, 0]
    mobile = mobility[0, 0][:, None, :]
    left_rows = pair_left[0, 0]
    right_rows = pair_right[0, 0]
    slot_rows = pair_slot[0, 0]
    live_count = pair_count[0, 0]
    own_blocks = jnp.concatenate([middles, halves[0, 0], burgers[0, 0]], axis=1)
    near_table = gather_near(own_blocks)
    force_one = evaluate(own_blocks, near_table, left_rows, right_rows, slot_rows, live_count)
    moved = middles + time_step * mobile * force_one
    moved_blocks = jnp.concatenate([moved, own_blocks[:, 3:]], axis=1)
    moved_table = gather_near(moved)
    second_table = jnp.concatenate([moved_table, near_table[:, :, 3:]], axis=2)
    force_two = evaluate(moved_blocks, second_table, left_rows, right_rows, slot_rows, live_count)
    final_midpoints = middles + 0.5 * time_step * mobile * (force_one + force_two)
    return (final_midpoints[None, None], force_two[None, None])


def solution(mesh):
    return jax.shard_map(
        on_device,
        mesh=mesh,
        in_specs=(
            P("gx", "gy", None, None, None),
            P("gx", "gy", None, None, None),
            P("gx", "gy", None, None, None),
            P("gx", "gy", None, None),
            P("gx", "gy", None),
            P("gx", "gy", None),
            P("gx", "gy", None),
            P("gx", "gy"),
        ),
        out_specs=(P("gx", "gy", None, None, None), P("gx", "gy", None, None, None)),
        check_vma=False,
    )
```

profile of v0, /device:TPU:1, one launch (start us, length us, event | category | flops | bytes accessed | tf_op | source)
XLA Modules:
  0.0 999.2 jit_solution(18428819079386188113)
XLA Ops:
  2.0 10.1 %collective-permute-done = f32[64,9,256]{2,0,1:T(8,128)S(1)} collective-permute-done((f32[64,9,256]{2,0,1:T(8,128)S(1)}, f32[64,9,256]{2,0,1:T(8,128)S(1)}, u32[]{:S(2)}, u32[]{:S(2)}) %collective-permute-start) | collective-permute-done | bytes 589856 | tf_op jit(solution)/shard_map/ppermute | solution.py:16
  18.6 35.4 %collective-permute-done.2 = f32[64,9,256]{2,0,1:T(8,128)S(1)} collective-permute-done((f32[64,9,256]{2,0,1:T(8,128)S(1)}, f32[64,9,256]{2,0,1:T(8,128)S(1)}, u32[]{:S(2)}, u32[]{:S(2)}) %collective-permute-start.2) | collective-permute-done | bytes 589856 | tf_op jit(solution)/shard_map/ppermute | solution.py:16
  59.9 376.2 %while.32 = (s32[]{:T(128)}, f32[64,3,256]{2,0,1:T(8,128)S(1)}, f32[256,3,256]{2,0,1:T(8,128)S(1)}, s32[]{:T(128)}, s32[128]{0:T(128)S(1)}, /*index=5*/s32[]{:T(...) while((s32[]{:T(128)}, f32[64,3,256]{2,0,1:T(8,128)S(1)}, ...), condition=%wide.region_27.30_spmd.clone.clone, body=%wide.region_0.29_spmd.clone.clone.sunk | while | flops 126863840 | bytes 30131980 | solution.py:137
  67.1 7.7 fusion.284
  90.6 7.7 fusion.284
  114.1 7.7 fusion.284
  137.7 7.7 fusion.284
  161.2 7.7 fusion.284
  184.7 7.7 fusion.284
  231.7 7.7 fusion.284
  255.2 7.7 fusion.284
  278.7 7.7 fusion.284
  302.2 7.7 fusion.284
  325.8 7.7 fusion.284
  349.3 7.7 fusion.284
  473.2 510.4 %while.33 = (s32[]{:T(128)}, f32[64,3,256]{2,0,1:T(8,128)S(1)}, f32[256,3,256]{2,0,1:T(8,128)S(1)}, s32[]{:T(128)}, s32[128]{0:T(128)S(1)}, /*index=5*/s32[]{:T(...) while((s32[]{:T(128)}, f32[64,3,256]{2,0,1:T(8,128)S(1)}, ...), condition=%wide.region_55.58_spmd.clone.clone, body=%wide.region_28.57_spmd.clone.clone.sunk | while | flops 126863840 | bytes 30310132 | solution.py:137
  487.6 8.6 fusion.298
  519.5 8.6 fusion.298
  551.4 8.6 fusion.298
  583.3 8.6 fusion.298
  615.2 8.6 fusion.298
  647.1 8.6 fusion.298
  679.0 8.6 fusion.298
  710.9 8.6 fusion.298
  742.8 8.6 fusion.298
  774.7 8.6 fusion.298
  806.6 8.6 fusion.298
  838.5 8.6 fusion.298
  870.4 8.6 fusion.298
  902.3 8.6 fusion.298
  934.2 8.6 fusion.298
  966.1 8.6 fusion.298
  (2126 shorter events, 708.5 us)
Async XLA Ops:
  1.9 10.2 %collective-permute-start = (f32[64,9,256]{2,0,1:T(8,128)S(1)}, f32[64,9,256]{2,0,1:T(8,128)S(1)}, u32[]{:S(2)}, u32[]{:S(2)}) collective-permute-start(f32[64,9,256]{2,0,1:T(8,128)S(1)} %get-tuple-element.712), channel_id=1, source_target_pairs={{0,24},{8,0},{16,8},{24,16},{1,25},{9,1},{17,9},{25,17},{2,26},{10... | collective-permute-start | bytes 1769480 | tf_op jit(solution)/shard_map/ppermute | solution.py:16
  13.3 40.8 %collective-permute-start.1 = (f32[2,64,9,256]{3,1,2,0:T(8,128)}, f32[2,64,9,256]{3,1,2,0:T(8,128)}, u32[]{:S(2)}, u32[]{:S(2)}) collective-permute-start(f32[2,64,9,256]{3,1,2,0:T(8,128)} %pad_maximum_fusion.2), channel_id=1, source_target_pairs={{0,7},{1,0},{2,1},{3,2},{4,3},{5,4},{6,5},{7,6},{8,15},{9,8},{10,9... | collective-permute-start | bytes 3538952 | tf_op jit(solution)/shard_map/ppermute | solution.py:16
  17.6 36.5 %collective-permute-start.2 = (f32[64,9,256]{2,0,1:T(8,128)S(1)}, f32[64,9,256]{2,0,1:T(8,128)S(1)}, u32[]{:S(2)}, u32[]{:S(2)}) collective-permute-start(f32[64,9,256]{2,0,1:T(8,128)S(1)} %collective-permute-done), channel_id=1, source_target_pairs={{0,1},{1,2},{2,3},{3,4},{4,5},{5,6},{6,7},{7,0},{8,9},{9,10},{10,1... | collective-permute-start | bytes 1769480 | tf_op jit(solution)/shard_map/ppermute | solution.py:16
  436.1 11.3 %copy-start.23 = (f32[1,1,64,256]{3,2,1,0:T(8,128)S(1)}, f32[1,1,64,256]{3,2,1,0:T(8,128)}, u32[]{:S(2)}) copy-start(f32[1,1,64,256]{3,2,1,0:T(8,128)} %param.19) | copy-start | bytes 196612
  436.1 14.3 %copy-start.5 = (f32[1,1,64,3,256]{4,2,3,1,0:T(8,128)S(1)}, f32[1,1,64,3,256]{4,2,3,1,0:T(8,128)}, u32[]{:S(2)}) copy-start(f32[1,1,64,3,256]{4,2,3,1,0:T(8,128)} %param.16) | copy-start | bytes 589828
  436.2 9.4 collective-permute-start.3
  436.3 6.8 collective-permute-start.4
  445.6 11.1 %copy-start.7 = (f32[2,64,3,256]{3,1,2,0:T(8,128)}, f32[2,64,3,256]{3,1,2,0:T(8,128)S(1)}, u32[]{:S(2)}) copy-start(f32[2,64,3,256]{3,1,2,0:T(8,128)S(1)} %collective-permute-done.3) | copy-start | bytes 1179652
  445.7 4.8 collective-permute-start.5
  450.4 8.7 copy-start.16
  450.5 6.2 collective-permute-start.6
  456.7 11.9 %collective-permute-start.7 = (f32[2,64,3,256]{3,1,2,0:T(8,128)S(1)}, f32[2,64,3,256]{3,1,2,0:T(8,128)S(1)}, u32[]{:S(2)}, u32[]{:S(2)}) collective-permute-start(f32[2,64,3,256]{3,1,2,0:T(8,128)S(1)} %pad_maximum_fusion.8), channel_id=1, source_target_pairs={{0,7},{1,0},{2,1},{3,2},{4,3},{5,4},{6,5},{7,6},{8,15},{9,8},{10,9... | collective-permute-start | bytes 1179656 | tf_op jit(solution)/shard_map/ppermute | solution.py:16
  459.1 9.5 collective-permute-start.8
  551.3 8.7 copy-start.9
  551.3 8.7 copy-start.10
  551.3 8.7 copy-start.11
  551.4 8.7 copy-start.12
  551.4 8.7 copy-start.13
  583.2 8.7 copy-start.9
  583.2 8.7 copy-start.10
  583.2 8.7 copy-start.11
  583.3 8.7 copy-start.12
  583.3 8.7 copy-start.13
  615.1 8.7 copy-start.9
  615.1 8.7 copy-start.10
  983.6 14.8 %copy-start.6 = (f32[1,1,64,3,256]{4,2,3,1,0:T(8,128)S(1)}, f32[1,1,64,3,256]{4,2,3,1,0:T(8,128)}, u32[]{:S(2)}) copy-start(f32[1,1,64,3,256]{4,2,3,1,0:T(8,128)} %param.16) | copy-start | bytes 589828
  983.6 14.7 %copy-start.8 = (f32[2,64,3,256]{3,1,2,0:T(8,128)S(1)}, f32[2,64,3,256]{3,1,2,0:T(8,128)}, u32[]{:S(2)}) copy-start(f32[2,64,3,256]{3,1,2,0:T(8,128)} %copy-done.7) | copy-start | bytes 1179652
  983.6 14.7 %copy-start.17 = (f32[64,3,256]{2,0,1:T(8,128)S(1)}, f32[64,3,256]{2,0,1:T(8,128)}, u32[]{:S(2)}) copy-start(f32[64,3,256]{2,0,1:T(8,128)} %copy-done.16) | copy-start | bytes 589828
  983.6 14.7 %copy-start.18 = (f32[64,256]{1,0:T(8,128)S(1)}, f32[64,256]{1,0:T(8,128)}, u32[]{:S(2)}) copy-start(f32[64,256]{1,0:T(8,128)} %get-tuple-element.714) | copy-start | bytes 196612
  983.7 9.4 collective-permute-start.9
  983.8 6.8 collective-permute-start.10
  993.1 5.2 collective-permute-start.11
  (410 other events, 2006.2 us)
where the time goes:
time: 1000 us; the launch traced here: 999 us
  matrix products  381 us (38%)
  other arithmetic  305 us (30%)
  local copies, waits for them, and re-layouts  203 us (20%)
  waiting for transfers between devices  74.4 us (7%)
  starting transfers between devices  19.6 us (2%)
  loops' own time  13.6 us (1%)
    dot_general x32, matrix products, pair_forces(): jnp.einsum('...ci,...cj->...ij', half_a, half_b, precision=lax.Precision....  260 us
    reduce_sum x32, other arithmetic, pair_forces(): jnp.sum(kernel * piece, axis=-2)  213 us
    gather x32, local copies, waits for them, and re-layouts, advance(): jnp.take(flat_table, table_place(kinds, layout) * block_count + second_id...  97.3 us
    ppermute x12, waiting for transfers between devices, from_behind(): lax.ppermute(x, axis, [(i, (i + by) % devices) for i in range(devices)])  74.4 us
    dot_general x32, matrix products, pair_forces(): jnp.einsum('...ci,...cj->...ij', burg_a, burg_b, precision=lax.Precision....  59.2 us
    while x1216, local copies, waits for them, and re-layouts  50 us
    dot_general x32, matrix products, advance(): jnp.einsum('gb,gcs->bcs', hot_back, force_b, precision=lax.Precision.HIGH...  33.7 us
    select_n x32, other arithmetic, advance(): outward = jnp.where(kinds > 0, active, 0.0)  29.1 us
  transfers between devices with their start and end apart: 12, of which 10 were waited for; matrix products, arithmetic and copies ran while one was open for 0% of the time, Pallas kernels for 0%

commit v1 on v0

v1 whole, which is shorter than its diff:
```python
import jax
import jax.numpy as jnp
from jax import lax
from jax.experimental import pallas as pl
from jax.experimental.pallas import tpu as pltpu
from jax.sharding import PartitionSpec as P

core_square = 0.04
poisson_part = 0.6
time_step = 0.1
gauss_offset = 0.5773502691896258
length_square = 1.5 * core_square
to_scaled = length_square**-0.5


def from_behind(x, axis, by):
    devices = lax.axis_size(axis)
    return lax.ppermute(x, axis, [(i, (i + by) % devices) for i in range(devices)])


def split_three(x):
    high = x.astype(jnp.bfloat16).astype(jnp.float32)
    rest = x - high
    middle = rest.astype(jnp.bfloat16).astype(jnp.float32)
    return high, middle, rest - middle


def prepare(k, ids, mid_ref, fixed_ref, buffers):
    cross_ref, couple_ref, column_ref, row_ref = buffers
    left_ref, right_ref, slot_ref = ids
    blocks = mid_ref.shape[0] // 5
    segments = mid_ref.shape[2]
    left = left_ref[k]
    kind = slot_ref[k]
    right = kind * blocks + right_ref[k]
    east = jnp.where((kind == 1) | (kind >= 3), 1.0, 0.0).astype(jnp.float32)
    north = jnp.where(
        (kind == 2) | (kind == 3), 1.0, jnp.where(kind == 4, -1.0, 0.0)
    ).astype(jnp.float32)
    component = lax.broadcasted_iota(jnp.int32, (3, segments), 0)
    offset = jnp.where(component == 0, east, jnp.where(component == 1, north, 0.0))
    mid_a = mid_ref[left] * to_scaled
    mid_b = (mid_ref[right] + offset) * to_scaled
    fixed_a = fixed_ref[left]
    fixed_b = fixed_ref[right]
    half_a, burg_a = fixed_a[:3], fixed_a[3:]
    half_b, burg_b = fixed_b[:3], fixed_b[3:]
    arm_a = half_a * (gauss_offset * to_scaled)
    arm_b = half_b * (gauss_offset * to_scaled)

    ones = jnp.ones((1, segments), jnp.float32)
    arm_square_a = jnp.sum(arm_a * arm_a, axis=0, keepdims=True)
    arm_square_b = jnp.sum(arm_b * arm_b, axis=0, keepdims=True)
    tilt_a = 2.0 * jnp.sum(mid_a * arm_a, axis=0, keepdims=True)
    tilt_b = 2.0 * jnp.sum(mid_b * arm_b, axis=0, keepdims=True)
    base_b = arm_square_b + core_square / length_square
    form_a = jnp.concatenate(
        [
            jnp.concatenate([-2.0 * arm_a, mid_a, arm_square_a + tilt_a, ones], axis=0),
            jnp.concatenate([2.0 * arm_a, mid_a, arm_square_a - tilt_a, ones], axis=0),
        ],
        axis=1,
    )
    form_b = jnp.concatenate(
        [
            jnp.concatenate([mid_b + arm_b, -2.0 * arm_b, ones, base_b + tilt_b], axis=0),
            jnp.concatenate([mid_b - arm_b, 2.0 * arm_b, ones, base_b - tilt_b], axis=0),
        ],
        axis=1,
    )
    high_a, middle_a, low_a = split_three(form_a)
    high_b, middle_b, low_b = split_three(form_b)
    wide_a = jnp.concatenate([high_a, high_a, middle_a, high_a, low_a, middle_a], axis=0)
    wide_b = jnp.concatenate([high_b, middle_b, high_b, low_b, high_b, middle_b], axis=0)
    cross_ref[...] = jnp.dot(
        jnp.transpose(wide_a).astype(jnp.bfloat16),
        wide_b.astype(jnp.bfloat16),
        preferred_element_type=jnp.float32,
    )

    screw_a = jnp.sum(burg_a * half_a, axis=0, keepdims=True) * poisson_part
    screw_b = jnp.sum(burg_b * half_b, axis=0, keepdims=True)
    blank = jnp.zeros((6, segments), jnp.float32)
    pair_a = jnp.concatenate(
        [burg_a[:1] * half_a, burg_a[1:2] * half_a, burg_a[2:] * half_a, screw_a, blank], axis=0
    )
    pair_b = jnp.concatenate(
        [burg_b[:1] * half_b, burg_b[1:2] * half_b, burg_b[2:] * half_b, screw_b, blank], axis=0
    ) * (1.0 / length_square)
    top_a = pair_a.astype(jnp.bfloat16).astype(jnp.float32)
    top_b = pair_b.astype(jnp.bfloat16).astype(jnp.float32)
    couple_ref[...] = jnp.dot(
        jnp.transpose(jnp.concatenate([top_a, top_a, pair_a - top_a], axis=0)).astype(jnp.bfloat16),
        jnp.concatenate([top_b, pair_b - top_b, top_b], axis=0).astype(jnp.bfloat16),
        preferred_element_type=jnp.float32,
    )
    spare = jnp.zeros((2, segments), jnp.float32)
    column_ref[...] = jnp.transpose(jnp.concatenate([mid_a, arm_a, spare], axis=0))
    row_ref[...] = jnp.concatenate([mid_b, arm_b, spare], axis=0)


def interact(k, live, ids, buffers, sum_ref, force_ref):
    cross_ref, couple_ref, column_ref, row_ref = buffers
    left_ref, right_ref, slot_ref = ids
    blocks = force_ref.shape[0] // 5
    segments = row_ref.shape[1]
    total_b = [jnp.zeros((8, segments), jnp.float32) for _ in range(3)]
    for top in range(0, segments, 8):
        gaps = [
            column_ref[top : top + 8, c : c + 1] - row_ref[c : c + 1, :] for c in range(3)
        ]
        square = gaps[0] * gaps[0] + gaps[1] * gaps[1] + gaps[2] * gaps[2]
        weights = []
        for start in (top, segments + top):
            for column in (0, segments):
                y = square + cross_ref[start : start + 8, column : column + segments]
                inverse = lax.rsqrt(y)
                inverse_square = inverse * inverse
                weights.append((inverse * inverse_square) * (1.0 + inverse_square))
        same_sum = weights[0] + weights[3]
        cross_sum = weights[1] + weights[2]
        same_gap = weights[0] - weights[3]
        cross_gap = weights[1] - weights[2]
        couple = couple_ref[top : top + 8, :]
        whole = couple * (same_sum + cross_sum)
        along_a = couple * (same_gap + cross_gap)
        along_b = couple * (same_gap - cross_gap)
        for c in range(3):
            force = (
                whole * gaps[c]
                + along_a * column_ref[top : top + 8, 3 + c : 4 + c]
                - along_b * row_ref[3 + c : 4 + c, :]
            )
            total_b[c] = total_b[c] + force
            folded = force[:, :128]
            for lane in range(128, segments, 128):
                folded = folded + force[:, lane : lane + 128]
            sum_ref[c * segments + top : c * segments + top + 8, :] = folded
    force_a = jnp.concatenate(
        [
            jnp.concatenate(
                [
                    jnp.sum(
                        jnp.transpose(
                            sum_ref[c * segments + lane : c * segments + lane + 128, :]
                        ),
                        axis=0,
                        keepdims=True,
                    )
                    for lane in range(0, segments, 128)
                ],
                axis=1,
            )
            for c in range(3)
        ],
        axis=0,
    )
    force_b = jnp.concatenate([jnp.sum(t, axis=0, keepdims=True) for t in total_b], axis=0)
    left = left_ref[k]
    kind = slot_ref[k]
    right = kind * blocks + right_ref[k]
    active = k < live
    force_ref[left] = force_ref[left] + jnp.where(active, force_a, 0.0)
    mutual = active & (left != right)
    force_ref[right] = force_ref[right] - jnp.where(mutual, force_b, 0.0)


def sweep_body(
    count_ref, left_ref, right_ref, slot_ref, mid_ref, fixed_ref, force_ref, *scratch
):
    even, odd = scratch[:4], scratch[4:8]
    even_sum, odd_sum = scratch[8:]
    ids = (left_ref, right_ref, slot_ref)
    live = count_ref[0]
    last = left_ref.shape[0] - 1
    force_ref[...] = jnp.zeros_like(force_ref)
    prepare(0, ids, mid_ref, fixed_ref, even)

    def advance(step, carry):
        first = 2 * step
        second = jnp.minimum(first + 1, last)
        third = jnp.minimum(first + 2, last)
        prepare(second, ids, mid_ref, fixed_ref, odd)
        interact(first, live, ids, even, even_sum, force_ref)
        prepare(third, ids, mid_ref, fixed_ref, even)
        live_second = jnp.where(first + 1 < live, live, 0)
        interact(second, live_second, ids, odd, odd_sum, force_ref)
        return carry

    lax.fori_loop(0, (live + 1) // 2, advance, 0)


def sweep(near_mids, near_fixed, left_rows, right_rows, slot_rows, live_count):
    segments = near_mids.shape[2]
    buffers = [
        pltpu.VMEM((2 * segments, 2 * segments), jnp.float32),
        pltpu.VMEM((segments, segments), jnp.float32),
        pltpu.VMEM((segments, 8), jnp.float32),
        pltpu.VMEM((8, segments), jnp.float32),
    ]
    sums = pltpu.VMEM((3 * segments, 128), jnp.float32)
    scalar = pl.BlockSpec(memory_space=pltpu.SMEM)
    vector = pl.BlockSpec(memory_space=pltpu.VMEM)
    return pl.pallas_call(
        sweep_body,
        name="pair_sweep",
        out_shape=jax.ShapeDtypeStruct(near_mids.shape, jnp.float32),
        in_specs=[scalar] * 4 + [vector] * 2,
        out_specs=vector,
        scratch_shapes=buffers + buffers + [sums, sums],
        compiler_params=pltpu.CompilerParams(vmem_limit_bytes=48 * 1024 * 1024),
    )(live_count, left_rows, right_rows, slot_rows, near_mids, near_fixed)


def gather_near(blocks):
    eastern = from_behind(blocks, "gx", -1)
    northern = from_behind(blocks, "gy", -1)
    north_east = from_behind(eastern, "gy", -1)
    south_east = from_behind(eastern, "gy", 1)
    return jnp.concatenate([blocks, eastern, northern, north_east, south_east])


def give_back(forces):
    own, eastern, northern, north_east, south_east = jnp.split(forces, 5)
    eastern = eastern + from_behind(north_east, "gy", 1) + from_behind(south_east, "gy", -1)
    return own + from_behind(northern, "gy", 1) + from_behind(eastern, "gx", 1)


def on_device(midpoints, halves, burgers, mobility, pair_left, pair_right, pair_slot, pair_count):
    middles = midpoints[0, 0]
    mobile = mobility[0, 0][:, None, :]
    pairs = (pair_left[0, 0], pair_right[0, 0], pair_slot[0, 0], pair_count[0])
    near_fixed = gather_near(jnp.concatenate([halves[0, 0], burgers[0, 0]], axis=1))
    near_mids = gather_near(middles)
    force_one = give_back(sweep(near_mids, near_fixed, *pairs))
    moved = middles + time_step * mobile * force_one
    force_two = give_back(sweep(gather_near(moved), near_fixed, *pairs))
    final_midpoints = middles + 0.5 * time_step * mobile * (force_one + force_two)
    return (final_midpoints[None, None], force_two[None, None])


def solution(mesh):
    return jax.shard_map(
        on_device,
        mesh=mesh,
        in_specs=(
            P("gx", "gy", None, None, None),
            P("gx", "gy", None, None, None),
            P("gx", "gy", None, None, None),
            P("gx", "gy", None, None),
            P("gx", "gy", None),
            P("gx", "gy", None),
            P("gx", "gy", None),
            P("gx", "gy"),
        ),
        out_specs=(P("gx", "gy", None, None, None), P("gx", "gy", None, None, None)),
        check_vma=False,
    )
```

time: 1000 us -> 338 us (0.34)
  matrix products: 381 us -> 0 us
  other arithmetic: 305 us -> 0.96 us
  local copies, waits for them, and re-layouts: 203 us -> 3.99 us
  starting transfers between devices: 19.6 us -> 196 us
  Pallas kernels: 0 us -> 76.5 us
  waiting for transfers between devices: 74.4 us -> 59.9 us
  loops' own time: 13.6 us -> 0 us
    dot_general x160 -> x0, matrix products: 381 us -> none  [the longest x32 260 us: pair_forces(): jnp.einsum('...ci,...cj->...ij', half_a, half_b, precision=lax.Precision....]
    reduce_sum x32 -> x0, other arithmetic: 213 us -> none  [pair_forces(): jnp.sum(kernel * piece, axis=-2)]
    ppermute x12 -> x20, starting transfers between devices: 19.6 us -> 196 us  [from_behind(): lax.ppermute(x, axis, [(i, (i + by) % devices) for i in range(devices)])]
    gather x64 -> x0, local copies, waits for them, and re-layouts: 115 us -> none  [the longest x32 97.3 us: advance(): jnp.take(flat_table, table_place(kinds, layout) * block_count + second_id...]
    pallas_call x0 -> x2, Pallas kernels: none -> 76.5 us  [sweep(): pl.pallas_call(sweep_body, name='pair_sweep', out_shape=jax.ShapeDtypeStr...]
    while x1216 -> x0, local copies, waits for them, and re-layouts: 50 us -> none
    select_n x160 -> x0, other arithmetic: 45 us -> none  [the longest x32 29.1 us: advance(): outward = jnp.where(kinds > 0, active, 0.0)]
    add x99 -> x2, other arithmetic: 28.3 us -> 0.18 us  [give_back(): eastern + from_behind(north_east, 'gy', 1)]
  transfers between devices with their start and end apart: 12 -> 20, of which waited for: 10 -> 14; matrix products, arithmetic and copies ran while one was open for 0% -> 0% of each run, Pallas kernels for 0% -> 0%
where the time goes in v1:
time: 338 us; the launch traced here: 339 us
  starting transfers between devices  196 us (58%)
  Pallas kernels  76.5 us (23%)
  waiting for transfers between devices  59.9 us (18%)
  local copies, waits for them, and re-layouts  3.99 us (1%)
    ppermute x20, starting transfers between devices, from_behind(): lax.ppermute(x, axis, [(i, (i + by) % devices) for i in range(devices)])  196 us
    pallas_call x2, Pallas kernels, sweep(): pl.pallas_call(sweep_body, name='pair_sweep', out_shape=jax.ShapeDtypeStr...  76.5 us
    ppermute x20, waiting for transfers between devices, from_behind(): lax.ppermute(x, axis, [(i, (i + by) % devices) for i in range(devices)])  59.9 us
  transfers between devices with their start and end apart: 20, of which 14 were waited for; matrix products, arithmetic and copies ran while one was open for 0% of the time, Pallas kernels for 0%

profile of v1, /device:TPU:1, one launch (start us, length us, event | category | flops | bytes accessed | tf_op | source)
XLA Modules:
  0.0 339.2 jit_solution(2626778923361309786)
XLA Ops:
  0.6 1.3 copy_bitcast_fusion
  2.2 5.8 %collective-permute-start.5 = (f32[64,6,256]{2,1,0:T(8,128)S(1)}, f32[64,6,256]{2,1,0:T(8,128)S(1)}, u32[]{:S(2)}, u32[]{:S(2)}) collective-permute-start(f32[64,6,256]{2,1,0:T(8,128)S(1)} %get-tuple-element.14), channel_id=1, source_target_pairs={{0,7},{1,0},{2,1},{3,2},{4,3},{5,4},{6,5},{7,6},{8,15},{9,8},{10,9... | collective-permute-start | bytes 1179656 | tf_op jit(solution)/shard_map/ppermute | solution.py:18
  8.1 1.3 collective-permute-start
  9.3 0.2 collective-permute-start.1
  10.4 4.4 %collective-permute-done = f32[64,3,256]{2,1,0:T(4,128)S(1)} collective-permute-done((f32[64,3,256]{2,1,0:T(4,128)S(1)}, f32[64,3,256]{2,1,0:T(4,128)S(1)}, u32[]{:S(2)}, u32[]{:S(2)}) %collective-permute-start) | collective-permute-done | bytes 196640 | tf_op jit(solution)/shard_map/ppermute | solution.py:18
  14.7 4.3 %collective-permute-start.2 = (f32[64,3,256]{2,1,0:T(4,128)S(1)}, f32[64,3,256]{2,1,0:T(4,128)S(1)}, u32[]{:S(2)}, u32[]{:S(2)}) collective-permute-start(f32[64,3,256]{2,1,0:T(4,128)S(1)} %collective-permute-done), channel_id=1, source_target_pairs={{0,7},{1,0},{2,1},{3,2},{4,3},{5,4},{6,5},{7,6},{8,15},{9,8},{10,9... | collective-permute-start | bytes 589832 | tf_op jit(solution)/shard_map/ppermute | solution.py:18
  19.1 4.8 %collective-permute-done.1 = f32[64,3,256]{2,1,0:T(4,128)S(1)} collective-permute-done((f32[64,3,256]{2,1,0:T(4,128)S(1)}, f32[64,3,256]{2,1,0:T(4,128)S(1)}, u32[]{:S(2)}, u32[]{:S(2)}) %collective-permute-start.1) | collective-permute-done | bytes 196640 | tf_op jit(solution)/shard_map/ppermute | solution.py:18
  24.0 5.9 %collective-permute-start.6 = (f32[64,6,256]{2,1,0:T(8,128)S(1)}, f32[64,6,256]{2,1,0:T(8,128)S(1)}, u32[]{:S(2)}, u32[]{:S(2)}) collective-permute-start(f32[64,6,256]{2,1,0:T(8,128)S(1)} %collective-permute-done.4), channel_id=1, source_target_pairs={{0,7},{1,0},{2,1},{3,2},{4,3},{5,4},{6,5},{7,6},{8,15},{9,8},{10,9... | collective-permute-start | bytes 1179656 | tf_op jit(solution)/shard_map/ppermute | solution.py:18
  29.9 2.7 collective-permute-done.2
  32.7 13.0 %collective-permute-done.3 = f32[64,3,256]{2,1,0:T(4,128)S(1)} collective-permute-done((f32[64,3,256]{2,1,0:T(4,128)S(1)}, f32[64,3,256]{2,1,0:T(4,128)S(1)}, u32[]{:S(2)}, u32[]{:S(2)}) %collective-permute-start.3) | collective-permute-done | bytes 196640 | tf_op jit(solution)/shard_map/ppermute | solution.py:18
  45.8 9.2 %collective-permute-done.6 = f32[64,6,256]{2,1,0:T(8,128)S(1)} collective-permute-done((f32[64,6,256]{2,1,0:T(8,128)S(1)}, f32[64,6,256]{2,1,0:T(8,128)S(1)}, u32[]{:S(2)}, u32[]{:S(2)}) %collective-permute-start.6) | collective-permute-done | bytes 393248 | tf_op jit(solution)/shard_map/ppermute | solution.py:18
  55.1 1.8 collective-permute-done.7
  56.9 38.3 %pair_sweep.2 = f32[320,3,256]{2,1,0:T(4,128)S(1)} custom-call(s32[1]{0:T(128)} %bitcast.26.count_ref, s32[128]{0:T(128)S(1)} %bitcast.28, s32[128]{0:T(128)S(1)} %bitcast.30, s32[128]{0:T(128)S(1)} %bitcast.32, f32[320,3,256]{2,1,0:T(4,128)S(1)} %constant_dynamic-update-slice_fusion.mid_ref, f32[320,6,256]{2,1,0:T(8,128)S(1)} %constant_dynamic-update-slice_fusion.5.fixed_ref), custom_call_target="tpu_custom_call" | custom-call | tf_op jit(solution)/shard_map/pair_sweep/pallas_call | solution.py:204
  95.4 2.0 collective-permute-start.10
  97.4 3.9 %collective-permute-start.8 = (f32[64,3,256]{2,1,0:T(4,128)S(1)}, f32[64,3,256]{2,1,0:T(4,128)S(1)}, u32[]{:S(2)}, u32[]{:S(2)}) collective-permute-start(f32[64,3,256]{2,1,0:T(4,128)S(1)} %get-tuple-element.11), channel_id=1, source_target_pairs={{0,1},{1,2},{2,3},{3,4},{4,5},{5,6},{6,7},{7,0},{8,9},{9,10},{10,1... | collective-permute-start | bytes 589832 | tf_op jit(solution)/shard_map/ppermute | solution.py:18
  101.3 4.0 %collective-permute-done.9 = f32[64,3,256]{2,1,0:T(4,128)S(1)} collective-permute-done((f32[64,3,256]{2,1,0:T(4,128)S(1)}, f32[64,3,256]{2,1,0:T(4,128)S(1)}, u32[]{:S(2)}, u32[]{:S(2)}) %collective-permute-start.9) | collective-permute-done | bytes 196640 | tf_op jit(solution)/shard_map/ppermute | solution.py:18
  105.4 79.1 %collective-permute-start.11 = (f32[64,3,256]{2,1,0:T(4,128)S(1)}, f32[64,3,256]{2,1,0:T(4,128)S(1)}, u32[]{:S(2)}, u32[]{:S(2)}) collective-permute-start(f32[64,3,256]{2,1,0:T(4,128)S(1)} %fusion.2), channel_id=1, source_target_pairs={{0,8},{8,16},{16,24},{24,0},{1,9},{9,17},{17,25},{25,1},{2,10},{10... | collective-permute-start | bytes 589832 | tf_op jit(solution)/shard_map/ppermute | solution.py:18
  184.5 4.0 %collective-permute-done.11 = f32[64,3,256]{2,1,0:T(4,128)S(1)} collective-permute-done((f32[64,3,256]{2,1,0:T(4,128)S(1)}, f32[64,3,256]{2,1,0:T(4,128)S(1)}, u32[]{:S(2)}, u32[]{:S(2)}) %collective-permute-start.11) | collective-permute-done | bytes 196640 | tf_op jit(solution)/shard_map/ppermute | solution.py:18
  188.5 0.3 constant_dynamic-update-slice_fusion.14
  188.9 5.7 %collective-permute-start.13 = (f32[64,3,256]{2,1,0:T(4,128)S(1)}, f32[64,3,256]{2,1,0:T(4,128)S(1)}, u32[]{:S(2)}, u32[]{:S(2)}) collective-permute-start(f32[64,3,256]{2,1,0:T(4,128)S(1)} %get-tuple-element.5), channel_id=1, source_target_pairs={{0,7},{1,0},{2,1},{3,2},{4,3},{5,4},{6,5},{7,6},{8,15},{9,8},{10,9... | collective-permute-start | bytes 589832 | tf_op jit(solution)/shard_map/ppermute | solution.py:18
  194.6 1.1 collective-permute-done.12
  195.7 5.7 %collective-permute-start.14 = (f32[64,3,256]{2,1,0:T(4,128)S(1)}, f32[64,3,256]{2,1,0:T(4,128)S(1)}, u32[]{:S(2)}, u32[]{:S(2)}) collective-permute-start(f32[64,3,256]{2,1,0:T(4,128)S(1)} %collective-permute-done.12), channel_id=1, source_target_pairs={{0,7},{1,0},{2,1},{3,2},{4,3},{5,4},{6,5},{7,6},{8,15},{9,8},{10,9... | collective-permute-start | bytes 589832 | tf_op jit(solution)/shard_map/ppermute | solution.py:18
  201.5 3.2 collective-permute-done.14
  204.7 4.5 %collective-permute-done.15 = f32[64,3,256]{2,1,0:T(4,128)S(1)} collective-permute-done((f32[64,3,256]{2,1,0:T(4,128)S(1)}, f32[64,3,256]{2,1,0:T(4,128)S(1)}, u32[]{:S(2)}, u32[]{:S(2)}) %collective-permute-start.15) | collective-permute-done | bytes 196640 | tf_op jit(solution)/shard_map/ppermute | solution.py:18
  209.3 38.3 %pair_sweep.3 = f32[320,3,256]{2,1,0:T(4,128)S(1)} custom-call(s32[1]{0:T(128)} %bitcast.27.count_ref, s32[128]{0:T(128)S(1)} %bitcast.29, s32[128]{0:T(128)S(1)} %bitcast.31, s32[128]{0:T(128)S(1)} %bitcast.33, f32[320,3,256]{2,1,0:T(4,128)S(1)} %constant_dynamic-update-slice_fusion.10.mid_ref, f32[320,6,256]{2,1,0:T(8,128)S(1)} %constant_dynamic-update-slice_fusion.5.fixed_ref), custom_call_target="tpu_custom_call" | custom-call | tf_op jit(solution)/shard_map/pair_sweep/pallas_call | solution.py:204
  247.8 4.1 %collective-permute-start.18 = (f32[64,3,256]{2,1,0:T(4,128)S(1)}, f32[64,3,256]{2,1,0:T(4,128)S(1)}, u32[]{:S(2)}, u32[]{:S(2)}) collective-permute-start(f32[64,3,256]{2,1,0:T(4,128)S(1)} %get-tuple-element.9), channel_id=1, source_target_pairs={{0,7},{1,0},{2,1},{3,2},{4,3},{5,4},{6,5},{7,6},{8,15},{9,8},{10,9... | collective-permute-start | bytes 589832 | tf_op jit(solution)/shard_map/ppermute | solution.py:18
  252.0 3.9 %collective-permute-done.17 = f32[64,3,256]{2,1,0:T(4,128)S(1)} collective-permute-done((f32[64,3,256]{2,1,0:T(4,128)S(1)}, f32[64,3,256]{2,1,0:T(4,128)S(1)}, u32[]{:S(2)}, u32[]{:S(2)}) %collective-permute-start.17) | collective-permute-done | bytes 196640 | tf_op jit(solution)/shard_map/ppermute | solution.py:18
  256.0 78.1 %collective-permute-start.19 = (f32[64,3,256]{2,1,0:T(4,128)S(1)}, f32[64,3,256]{2,1,0:T(4,128)S(1)}, u32[]{:S(2)}, u32[]{:S(2)}) collective-permute-start(f32[64,3,256]{2,1,0:T(4,128)S(1)} %fusion), channel_id=1, source_target_pairs={{0,8},{8,16},{16,24},{24,0},{1,9},{9,17},{17,25},{25,1},{2,10},{10... | collective-permute-start | bytes 589832 | tf_op jit(solution)/shard_map/ppermute | solution.py:18
  334.1 3.3 collective-permute-done.19
  337.4 0.4 fusion.4
  337.8 0.7 copy.13
  338.5 0.7 copy.14
  (45 shorter events, 1.8 us)
Async XLA Ops:
  0.6 7.3 %copy-start.3 = (f32[1,1,64,3,256]{4,2,3,1,0:T(8,128)S(1)}, f32[1,1,64,3,256]{4,2,3,1,0:T(8,128)}, u32[]{:S(2)}) copy-start(f32[1,1,64,3,256]{4,2,3,1,0:T(8,128)} %param.8) | copy-start | bytes 589828
  2.1 21.9 %collective-permute-start.4 = (f32[64,6,256]{2,1,0:T(8,128)S(1)}, f32[64,6,256]{2,1,0:T(8,128)S(1)}, u32[]{:S(2)}, u32[]{:S(2)}) collective-permute-start(f32[64,6,256]{2,1,0:T(8,128)S(1)} %get-tuple-element.14), channel_id=1, source_target_pairs={{0,24},{8,0},{16,8},{24,16},{1,25},{9,1},{17,9},{25,17},{2,26},{10... | collective-permute-start | bytes 1179656 | tf_op jit(solution)/shard_map/ppermute | solution.py:18
  2.2 43.6 %collective-permute-start.5 = (f32[64,6,256]{2,1,0:T(8,128)S(1)}, f32[64,6,256]{2,1,0:T(8,128)S(1)}, u32[]{:S(2)}, u32[]{:S(2)}) collective-permute-start(f32[64,6,256]{2,1,0:T(8,128)S(1)} %get-tuple-element.14), channel_id=1, source_target_pairs={{0,7},{1,0},{2,1},{3,2},{4,3},{5,4},{6,5},{7,6},{8,15},{9,8},{10,9... | collective-permute-start | bytes 1179656 | tf_op jit(solution)/shard_map/ppermute | solution.py:18
  8.1 6.6 %collective-permute-start = (f32[64,3,256]{2,1,0:T(4,128)S(1)}, f32[64,3,256]{2,1,0:T(4,128)S(1)}, u32[]{:S(2)}, u32[]{:S(2)}) collective-permute-start(f32[64,3,256]{2,1,0:T(4,128)S(1)} %bitcast.34), channel_id=1, source_target_pairs={{0,24},{8,0},{16,8},{24,16},{1,25},{9,1},{17,9},{25,17},{2,26},{10... | collective-permute-start | bytes 589832 | tf_op jit(solution)/shard_map/ppermute | solution.py:18
  9.3 14.6 %collective-permute-start.1 = (f32[64,3,256]{2,1,0:T(4,128)S(1)}, f32[64,3,256]{2,1,0:T(4,128)S(1)}, u32[]{:S(2)}, u32[]{:S(2)}) collective-permute-start(f32[64,3,256]{2,1,0:T(4,128)S(1)} %bitcast.35), channel_id=1, source_target_pairs={{0,7},{1,0},{2,1},{3,2},{4,3},{5,4},{6,5},{7,6},{8,15},{9,8},{10,9... | collective-permute-start | bytes 589832 | tf_op jit(solution)/shard_map/ppermute | solution.py:18
  14.7 17.9 %collective-permute-start.2 = (f32[64,3,256]{2,1,0:T(4,128)S(1)}, f32[64,3,256]{2,1,0:T(4,128)S(1)}, u32[]{:S(2)}, u32[]{:S(2)}) collective-permute-start(f32[64,3,256]{2,1,0:T(4,128)S(1)} %collective-permute-done), channel_id=1, source_target_pairs={{0,7},{1,0},{2,1},{3,2},{4,3},{5,4},{6,5},{7,6},{8,15},{9,8},{10,9... | collective-permute-start | bytes 589832 | tf_op jit(solution)/shard_map/ppermute | solution.py:18
  19.0 26.6 %collective-permute-start.3 = (f32[64,3,256]{2,1,0:T(4,128)S(1)}, f32[64,3,256]{2,1,0:T(4,128)S(1)}, u32[]{:S(2)}, u32[]{:S(2)}) collective-permute-start(f32[64,3,256]{2,1,0:T(4,128)S(1)} %collective-permute-done), channel_id=1, source_target_pairs={{0,1},{1,2},{2,3},{3,4},{4,5},{5,6},{6,7},{7,0},{8,9},{9,10},{10,1... | collective-permute-start | bytes 589832 | tf_op jit(solution)/shard_map/ppermute | solution.py:18
  24.0 31.1 %collective-permute-start.6 = (f32[64,6,256]{2,1,0:T(8,128)S(1)}, f32[64,6,256]{2,1,0:T(8,128)S(1)}, u32[]{:S(2)}, u32[]{:S(2)}) collective-permute-start(f32[64,6,256]{2,1,0:T(8,128)S(1)} %collective-permute-done.4), channel_id=1, source_target_pairs={{0,7},{1,0},{2,1},{3,2},{4,3},{5,4},{6,5},{7,6},{8,15},{9,8},{10,9... | collective-permute-start | bytes 1179656 | tf_op jit(solution)/shard_map/ppermute | solution.py:18
  29.9 27.0 %collective-permute-start.7 = (f32[64,6,256]{2,1,0:T(8,128)S(1)}, f32[64,6,256]{2,1,0:T(8,128)S(1)}, u32[]{:S(2)}, u32[]{:S(2)}) collective-permute-start(f32[64,6,256]{2,1,0:T(8,128)S(1)} %collective-permute-done.4), channel_id=1, source_target_pairs={{0,1},{1,2},{2,3},{3,4},{4,5},{5,6},{6,7},{7,0},{8,9},{9,10},{10,1... | collective-permute-start | bytes 1179656 | tf_op jit(solution)/shard_map/ppermute | solution.py:18
  45.8 11.1 %copy-start = (s32[1,1,128]{2,1,0:T(1,128)S(1)}, s32[1,1,128]{2,1,0:T(1,128)}, u32[]{:S(2)}) copy-start(s32[1,1,128]{2,1,0:T(1,128)} %param.12) | copy-start | bytes 1540
  45.8 11.1 %copy-start.1 = (s32[1,1,128]{2,1,0:T(1,128)S(1)}, s32[1,1,128]{2,1,0:T(1,128)}, u32[]{:S(2)}) copy-start(s32[1,1,128]{2,1,0:T(1,128)} %param.13) | copy-start | bytes 1540
  45.8 11.1 %copy-start.2 = (s32[1,1,128]{2,1,0:T(1,128)S(1)}, s32[1,1,128]{2,1,0:T(1,128)}, u32[]{:S(2)}) copy-start(s32[1,1,128]{2,1,0:T(1,128)} %param.14) | copy-start | bytes 1540
  95.2 89.2 %copy-start.4 = (f32[1,1,64,256]{3,2,1,0:T(8,128)S(1)}, f32[1,1,64,256]{3,2,1,0:T(8,128)}, u32[]{:S(2)}) copy-start(f32[1,1,64,256]{3,2,1,0:T(8,128)} %param.11) | copy-start | bytes 196612
  95.4 5.9 %collective-permute-start.10 = (f32[64,3,256]{2,1,0:T(4,128)S(1)}, f32[64,3,256]{2,1,0:T(4,128)S(1)}, u32[]{:S(2)}, u32[]{:S(2)}) collective-permute-start(f32[64,3,256]{2,1,0:T(4,128)S(1)} %get-tuple-element.12), channel_id=1, source_target_pairs={{0,7},{1,0},{2,1},{3,2},{4,3},{5,4},{6,5},{7,6},{8,15},{9,8},{10,9... | collective-permute-start | bytes 589832 | tf_op jit(solution)/shard_map/ppermute | solution.py:18
  97.4 7.9 %collective-permute-start.9 = (f32[64,3,256]{2,1,0:T(4,128)S(1)}, f32[64,3,256]{2,1,0:T(4,128)S(1)}, u32[]{:S(2)}, u32[]{:S(2)}) collective-permute-start(f32[64,3,256]{2,1,0:T(4,128)S(1)} %get-tuple-element.13), channel_id=1, source_target_pairs={{0,1},{1,2},{2,3},{3,4},{4,5},{5,6},{6,7},{7,0},{8,9},{9,10},{10,1... | collective-permute-start | bytes 589832 | tf_op jit(solution)/shard_map/ppermute | solution.py:18
  97.4 87.1 %collective-permute-start.8 = (f32[64,3,256]{2,1,0:T(4,128)S(1)}, f32[64,3,256]{2,1,0:T(4,128)S(1)}, u32[]{:S(2)}, u32[]{:S(2)}) collective-permute-start(f32[64,3,256]{2,1,0:T(4,128)S(1)} %get-tuple-element.11), channel_id=1, source_target_pairs={{0,1},{1,2},{2,3},{3,4},{4,5},{5,6},{6,7},{7,0},{8,9},{9,10},{10,1... | collective-permute-start | bytes 589832 | tf_op jit(solution)/shard_map/ppermute | solution.py:18
  105.4 83.1 %collective-permute-start.11 = (f32[64,3,256]{2,1,0:T(4,128)S(1)}, f32[64,3,256]{2,1,0:T(4,128)S(1)}, u32[]{:S(2)}, u32[]{:S(2)}) collective-permute-start(f32[64,3,256]{2,1,0:T(4,128)S(1)} %fusion.2), channel_id=1, source_target_pairs={{0,8},{8,16},{16,24},{24,0},{1,9},{9,17},{17,25},{25,1},{2,10},{10... | collective-permute-start | bytes 589832 | tf_op jit(solution)/shard_map/ppermute | solution.py:18
  188.8 6.9 %collective-permute-start.12 = (f32[64,3,256]{2,1,0:T(4,128)S(1)}, f32[64,3,256]{2,1,0:T(4,128)S(1)}, u32[]{:S(2)}, u32[]{:S(2)}) collective-permute-start(f32[64,3,256]{2,1,0:T(4,128)S(1)} %get-tuple-element.5), channel_id=1, source_target_pairs={{0,24},{8,0},{16,8},{24,16},{1,25},{9,1},{17,9},{25,17},{2,26},{10... | collective-permute-start | bytes 589832 | tf_op jit(solution)/shard_map/ppermute | solution.py:18
  188.9 12.6 %collective-permute-start.13 = (f32[64,3,256]{2,1,0:T(4,128)S(1)}, f32[64,3,256]{2,1,0:T(4,128)S(1)}, u32[]{:S(2)}, u32[]{:S(2)}) collective-permute-start(f32[64,3,256]{2,1,0:T(4,128)S(1)} %get-tuple-element.5), channel_id=1, source_target_pairs={{0,7},{1,0},{2,1},{3,2},{4,3},{5,4},{6,5},{7,6},{8,15},{9,8},{10,9... | collective-permute-start | bytes 589832 | tf_op jit(solution)/shard_map/ppermute | solution.py:18
  195.7 9.0 %collective-permute-start.14 = (f32[64,3,256]{2,1,0:T(4,128)S(1)}, f32[64,3,256]{2,1,0:T(4,128)S(1)}, u32[]{:S(2)}, u32[]{:S(2)}) collective-permute-start(f32[64,3,256]{2,1,0:T(4,128)S(1)} %collective-permute-done.12), channel_id=1, source_target_pairs={{0,7},{1,0},{2,1},{3,2},{4,3},{5,4},{6,5},{7,6},{8,15},{9,8},{10,9... | collective-permute-start | bytes 589832 | tf_op jit(solution)/shard_map/ppermute | solution.py:18
  201.4 7.9 %collective-permute-start.15 = (f32[64,3,256]{2,1,0:T(4,128)S(1)}, f32[64,3,256]{2,1,0:T(4,128)S(1)}, u32[]{:S(2)}, u32[]{:S(2)}) collective-permute-start(f32[64,3,256]{2,1,0:T(4,128)S(1)} %collective-permute-done.12), channel_id=1, source_target_pairs={{0,1},{1,2},{2,3},{3,4},{4,5},{5,6},{6,7},{7,0},{8,9},{9,10},{10,1... | collective-permute-start | bytes 589832 | tf_op jit(solution)/shard_map/ppermute | solution.py:18
  247.8 8.1 %collective-permute-start.17 = (f32[64,3,256]{2,1,0:T(4,128)S(1)}, f32[64,3,256]{2,1,0:T(4,128)S(1)}, u32[]{:S(2)}, u32[]{:S(2)}) collective-permute-start(f32[64,3,256]{2,1,0:T(4,128)S(1)} %get-tuple-element.10), channel_id=1, source_target_pairs={{0,1},{1,2},{2,3},{3,4},{4,5},{5,6},{6,7},{7,0},{8,9},{9,10},{10,1... | collective-permute-start | bytes 589832 | tf_op jit(solution)/shard_map/ppermute | solution.py:18
  247.8 8.1 %collective-permute-start.18 = (f32[64,3,256]{2,1,0:T(4,128)S(1)}, f32[64,3,256]{2,1,0:T(4,128)S(1)}, u32[]{:S(2)}, u32[]{:S(2)}) collective-permute-start(f32[64,3,256]{2,1,0:T(4,128)S(1)} %get-tuple-element.9), channel_id=1, source_target_pairs={{0,7},{1,0},{2,1},{3,2},{4,3},{5,4},{6,5},{7,6},{8,15},{9,8},{10,9... | collective-permute-start | bytes 589832 | tf_op jit(solution)/shard_map/ppermute | solution.py:18
  252.0 82.1 %collective-permute-start.16 = (f32[64,3,256]{2,1,0:T(4,128)S(1)}, f32[64,3,256]{2,1,0:T(4,128)S(1)}, u32[]{:S(2)}, u32[]{:S(2)}) collective-permute-start(f32[64,3,256]{2,1,0:T(4,128)S(1)} %get-tuple-element.8), channel_id=1, source_target_pairs={{0,1},{1,2},{2,3},{3,4},{4,5},{5,6},{6,7},{7,0},{8,9},{9,10},{10,1... | collective-permute-start | bytes 589832 | tf_op jit(solution)/shard_map/ppermute | solution.py:18
  256.0 81.4 %collective-permute-start.19 = (f32[64,3,256]{2,1,0:T(4,128)S(1)}, f32[64,3,256]{2,1,0:T(4,128)S(1)}, u32[]{:S(2)}, u32[]{:S(2)}) collective-permute-start(f32[64,3,256]{2,1,0:T(4,128)S(1)} %fusion), channel_id=1, source_target_pairs={{0,8},{8,16},{16,24},{24,0},{1,9},{9,17},{17,25},{25,1},{2,10},{10... | collective-permute-start | bytes 589832 | tf_op jit(solution)/shard_map/ppermute | solution.py:18
